TPU v7x, 8 devices: a whole 2x2x1 slice. The times are simulated.
8 devices in a mesh: rep: 1 (over z), r: 2 (over y), s: 4 (over x, core).
Axes of the slice: x: 2, y: 2, z: 1, core: 2. Of those that a mesh axis runs over, the one named last changes fastest.
Arguments:
- x: bfloat16 [8, 4096, 896], P(('rep', 'r', 's'))
- dy: bfloat16 [8, 4096, 896], P(('rep', 'r', 's'))
- w_gate: bfloat16 [2, 896, 2560], P(None, 's')
- w_up: bfloat16 [2, 896, 2560], P(None, 's')
- w_down: bfloat16 [2, 2560, 896], P(None, 's')
- m_w_gate: float32 [2, 896, 2560], P(None, 's')
- m_w_up: float32 [2, 896, 2560], P(None, 's')
- m_w_down: float32 [2, 2560, 896], P(None, 's')
- v_w_gate: float32 [2, 896, 2560], P(None, 's')
- v_w_up: float32 [2, 896, 2560], P(None, 's')
- v_w_down: float32 [2, 2560, 896], P(None, 's')
Outputs:
- output 1: bfloat16 [2, 896, 2560], P('rep', 's')
- output 2: bfloat16 [2, 896, 2560], P('rep', 's')
- output 3: bfloat16 [2, 2560, 896], P('rep', 's')
- output 4: float32 [2, 896, 2560], P('rep', 's')
- output 5: float32 [2, 896, 2560], P('rep', 's')
- output 6: float32 [2, 2560, 896], P('rep', 's')
- output 7: float32 [2, 896, 2560], P('rep', 's')
- output 8: float32 [2, 896, 2560], P('rep', 's')
- output 9: float32 [2, 2560, 896], P('rep', 's')
All inputs are finite; a program needn't handle non-finite values.
Results may differ from a plain program's by a relative error of at most 0.022.
Values are sent between devices in bfloat16 or wider.
A program may use at most 2 GiB of HBM per device.

v0:
```python
import jax
import jax.numpy as jnp
from jax import lax
from jax.sharding import PartitionSpec as P

NAMES = ("w_gate", "w_up", "w_down")


def matmul(a, w):
    return jnp.dot(a, w, preferred_element_type=jnp.float32).astype(jnp.bfloat16)


def normed(h):
    wide = h.astype(jnp.float32)
    scale = lax.rsqrt(jnp.mean(wide**2, -1, keepdims=True) + 1e-6)
    return (wide * scale).astype(jnp.bfloat16)


def layer(h, w):
    a = normed(h)
    gate = jnp.dot(a, w["w_gate"], preferred_element_type=jnp.float32)
    up = jnp.dot(a, w["w_up"], preferred_element_type=jnp.float32)
    return h + matmul((jax.nn.silu(gate) * up).astype(jnp.bfloat16), w["w_down"])


def adamw(w, m, v, g):
    m = 0.9 * m + 0.1 * g
    v = 0.95 * v + 0.05 * g * g
    step = m * lax.rsqrt(v + 1e-8) + 0.1 * w
    return (w - 0.02 * step).astype(jnp.bfloat16), m, v


def clipped(gradients, sum_of_squares, count):
    factor = jnp.minimum(1.0, 0.5 * lax.rsqrt(sum_of_squares / count + 1e-30))
    return [g * factor for g in gradients]


def solution(mesh):
    def fetched(weights, number):
        return {name: lax.all_gather(w[number], "s", axis=0, tiled=True) for name, w in zip(NAMES, weights, strict=True)}

    def summed(term):
        return lax.psum(lax.psum_scatter(term, "s", scatter_dimension=0, tiled=True), "r")

    def step(x, dy, *arrays):
        weights, m, v = (arrays[i : i + 3] for i in (0, 3, 6))
        layers = weights[0].shape[0]
        h, kept = x[0], []
        for number in range(layers):
            kept.append(h)
            h = layer(h, fetched(weights, number))
        by_h, mine = dy[0], [None] * layers
        for number in reversed(range(layers)):
            _, back = jax.vjp(lambda w, h: layer(h, w), fetched(weights, number), kept[number])
            by_w, by_h = back(by_h)
            mine[number] = [summed(by_w[name]) for name in NAMES]
        gradients = [jnp.stack([mine[number][i] for number in range(layers)]).astype(jnp.float32) for i in range(3)]
        squares = lax.psum(sum(jnp.sum(g * g) for g in gradients), "s")
        gradients = clipped(gradients, squares, lax.psum(1, "s") * sum(g.size for g in gradients))
        new = [adamw(w.astype(jnp.float32), m, v, g) for w, m, v, g in zip(weights, m, v, gradients, strict=True)]
        return tuple(one[which] for which in range(3) for one in new)

    states, cut = P(("rep", "r", "s"), None, None), P(None, "s", None)
    return jax.shard_map(
        step,
        mesh=mesh,
        in_specs=(states, states) + (cut,) * 9,
        out_specs=(P("rep", "s", None),) * 9,
        check_vma=False,
    )
```

profile of v0, /device:TPU:0, one launch (start us, length us, event | category | flops | bytes accessed | tf_op | source)
XLA Modules:
  0.0 870.4 jit_solution(5250709855326562594)
XLA Ops:
  7.2 0.0 all-gather.13.cloned.1.call-start
  7.2 3.3 fusion.91
  10.5 0.0 all-gather.13.cloned.1.call-update
  10.5 0.0 all-gather.15.cloned.1.call-start
  10.6 3.1 fusion.90
  13.7 0.0 all-gather.15.cloned.1.call-update
  13.8 0.0 all-gather.17.cloned.1.call-start
  13.8 1.6 fusion.89
  15.4 0.0 all-gather.17.cloned.1.call-update
  15.4 0.0 all-gather.23.cloned.1.call-start
  15.4 0.5 all-gather.23.cloned.1.call-update
  16.0 0.0 all-gather.21.cloned.1.call-start
  16.0 0.5 all-gather.21.cloned.1.call-update
  16.6 0.0 all-gather.19.cloned.1.call-start
  16.6 0.5 all-gather.19.cloned.1.call-update
  17.1 0.0 reduce-scatter.15.cloned.1.call-start
  17.2 10.8 %copy.20 = bf16[1,4096,896]{1,2,0:T(8,128)(2,1)} copy(bf16[1,4096,896]{2,1,0:T(8,128)(2,1)} %param.11) | data formatting | bytes 14680064 | tf_op args[0]
  28.0 4.6 fusion.15
  32.5 10.7 %copy.21 = bf16[1,4096,896]{1,2,0:T(8,128)(2,1)} copy(bf16[1,4096,896]{2,1,0:T(8,128)(2,1)} %param.12) | data formatting | bytes 14680064 | tf_op args[1]
  43.2 4.1 all-gather.13.cloned.1.call-done
  47.3 29.4 %fusion.47 = f32[4096,2560]{1,0:T(8,128)} fusion(bf16[1,4096,896]{1,2,0:T(8,128)(2,1)} %copy.20, f32[4096]{0:T(1024)S(1)} %add_rsqrt_fusion, bf16[1,896,2560]{2,1,0:T(8,128)(2,1)} %all-gather.13.cloned.1.call-done), kind=kOutput, calls=%fused_computation.72 | convolution fusion | flops 18801491968 | bytes 53886976 | tf_op jit(solution)/shard_map/dot_general | solution.py:21
  76.7 6.5 all-gather.15.cloned.1.call-done
  83.2 49.7 %multiply_convert_fusion.1 = (bf16[4096,2560]{1,0:T(8,128)(2,1)}, f32[4096,2560]{1,0:T(8,128)}) fusion(f32[4096,2560]{1,0:T(8,128)} %fusion.47, bf16[1,896,2560]{2,1,0:T(8,128)(2,1)} %all-gather.15.cloned.1.call-done, bf16[1,4096,896]{1,2,0:T(8,128)(2,1)} %copy.20, f32[4096]{0:T(1024)S(1)} %add_rsqrt_fusion), kind=kOutput, calls=%fused_computation.17 | convolution fusion | flops 18864406528 | bytes 116801536 | tf_op jit(solution)/shard_map/dot_general | solution.py:22
  132.9 26.8 %fusion.19 = (f32[4096]{0:T(1024)S(1)}, bf16[4096,896]{0,1:T(8,128)(2,1)}) fusion(bf16[4096,2560]{1,0:T(8,128)(2,1)} %get-tuple-element.30, bf16[1,2560,896]{2,1,0:T(8,128)(2,1)} %all-gather.17.cloned.1.call-done, bf16[1,4096,896]{1,2,0:T(8,128)(2,1)} %copy.20), kind=kOutput, calls=%fused_computation.37 | convolution fusion | flops 18808827904 | bytes 40255488 | tf_op jit(solution)/shard_map/dot_general | solution.py:10
  159.7 0.6 copy-done.7
  160.4 0.0 all-gather.23.cloned.1.call-done
  160.4 29.6 %fusion.39 = f32[4096,2560]{1,0:T(8,128)} fusion(bf16[4096,896]{0,1:T(8,128)(2,1)} %get-tuple-element.33, f32[4096]{0:T(1024)S(1)} %fusion.77, bf16[1,896,2560]{2,1,0:T(8,128)(2,1)} %all-gather.23.cloned.1.call-done), kind=kOutput, calls=%fused_computation.69 | convolution fusion | flops 18801491968 | bytes 53886976 | tf_op jit(solution)/shard_map/jvp()/dot_general | solution.py:22
  190.0 0.6 all-gather.21.cloned.1.call-done
  190.6 28.4 %convolution_convert_fusion.1 = bf16[4096,2560]{1,0:T(8,128)(2,1)} fusion(bf16[1,4096,896]{2,1,0:T(8,128)(2,1)} %param.12, bf16[1,2560,896]{2,1,0:T(8,128)(2,1)} %all-gather.21.cloned.1.call-done), kind=kOutput, calls=%fused_computation.27 | convolution fusion | flops 18800967680 | bytes 32899072 | tf_op jit(solution)/shard_map/transpose(jvp())/dot_general | solution.py:10
  219.1 7.4 all-gather.19.cloned.1.call-done
  226.4 58.3 %fusion.2 = (bf16[4096,2560]{1,0:T(8,128)(2,1)}, f32[4096,2560]{1,0:T(8,128)}) fusion(f32[4096,2560]{1,0:T(8,128)} %fusion.39, bf16[4096,2560]{1,0:T(8,128)(2,1)} %convolution_convert_fusion.1, bf16[1,896,2560]{2,1,0:T(8,128)(2,1)} %all-gather.19.cloned.1.call-done, bf16[4096,896]{0,1:T(8,128)(2,1)} %get-tuple-element.33, f32[4096]{0:T(1024)S(1)} %fusion.77), kind=kOutput, calls=%fused_computation.8 | convolution fusion | flops 18927321088 | bytes 137773056 | tf_op jit(solution)/shard_map/jvp()/dot_general | solution.py:21
  284.8 23.6 %fusion.70 = bf16[4096,896]{0,1:T(8,128)(2,1)} fusion(bf16[4096,2560]{1,0:T(8,128)(2,1)} %get-tuple-element.34, bf16[1,896,2560]{2,1,0:T(8,128)(2,1)S(1)} %copy-done.11), kind=kOutput, calls=%fused_computation.94 | convolution fusion | flops 18790481920 | bytes 32899072 | tf_op jit(solution)/shard_map/transpose(jvp())/dot_general | solution.py:21
  308.3 38.7 %fusion.21 = (f32[4096]{0:T(1024)S(1)}, bf16[4096,896]{0,1:T(8,128)(2,1)}) fusion(bf16[4096,896]{0,1:T(8,128)(2,1)} %get-tuple-element.33, bf16[4096,896]{0,1:T(8,128)(2,1)} %fusion.70, bf16[1,896,2560]{2,1,0:T(8,128)(2,1)} %all-gather.23.cloned.1.call-done, bf16[4096,2560]{1,0:T(8,128)(2,1)} %convolution_convert_fusion.1, f32[4096,2560]{1,0:T(8,128)} %get-tuple-element.35), kind=kOutput, calls=%fused_computation.39 | convolution fusion | flops 18875412480 | bytes 89538560 | tf_op jit(solution)/shard_map/transpose(jvp())/dot_general | solution.py:22
  347.1 9.8 %fusion.22 = bf16[4096,896]{0,1:T(8,128)(2,1)S(1)} fusion(bf16[4096,896]{0,1:T(8,128)(2,1)} %get-tuple-element.33, bf16[4096,896]{0,1:T(8,128)(2,1)} %get-tuple-element.37, bf16[1,4096,896]{1,2,0:T(8,128)(2,1)} %copy.21, f32[4096]{0:T(1024)S(1)} %multiply_multiply_fusion.3, f32[4096]{0:T(1024)S(1)} %fusion.77), kind=kLoop, calls=%fused_computation.40 | loop fusion | flops 25690112 | bytes 29392896 | tf_op jit(solution)/shard_map/transpose(jvp())/add_any | solution.py:14
  356.9 3.0 copy-done.3
  359.9 26.4 %convolution_convert_fusion.2 = bf16[2560,896]{1,0:T(8,128)(2,1)} fusion(bf16[4096,2560]{1,0:T(8,128)(2,1)} %get-tuple-element.30, bf16[4096,896]{0,1:T(8,128)(2,1)S(1)} %fusion.22), kind=kOutput, calls=%fused_computation.67 | convolution fusion | flops 18792775680 | bytes 32899072 | tf_op jit(solution)/shard_map/transpose(jvp())/dot_general | solution.py:10
  386.3 0.0 reduce-scatter.15.cloned.1.call-update
  386.3 0.0 reduce-scatter.17.cloned.1.call-start
  386.3 36.2 %fusion.29 = bf16[2560,896]{1,0:T(8,128)(2,1)} fusion(bf16[1,4096,896]{2,1,0:T(8,128)(2,1)} %param.12, f32[4096,2560]{1,0:T(8,128)} %fusion.39, f32[4096,2560]{1,0:T(8,128)} %get-tuple-element.35), kind=kOutput, calls=%fused_computation.63 | convolution fusion | flops 18855690240 | bytes 95813632 | tf_op jit(solution)/shard_map/transpose(jvp())/dot_general | solution.py:10
  422.6 0.0 reduce-scatter.17.cloned.1.call-update
  422.6 0.0 reduce-scatter.11.cloned.1.call-start
  422.6 27.7 %convolution_convert_fusion = bf16[4096,2560]{1,0:T(8,128)(2,1)} fusion(bf16[4096,896]{0,1:T(8,128)(2,1)} %copy-done.3, bf16[1,2560,896]{2,1,0:T(8,128)(2,1)} %all-gather.17.cloned.1.call-done), kind=kOutput, calls=%fused_computation.26 | convolution fusion | flops 18800967680 | bytes 32899072 | tf_op jit(solution)/shard_map/transpose(jvp())/dot_general | solution.py:10
  450.4 34.1 %fusion.36 = bf16[896,2560]{1,0:T(8,128)(2,1)} fusion(bf16[4096,2560]{1,0:T(8,128)(2,1)} %convolution_convert_fusion, f32[4096,2560]{1,0:T(8,128)} %fusion.47, bf16[1,4096,896]{1,2,0:T(8,128)(2,1)} %copy.20, f32[4096]{0:T(1024)S(1)} %copy-done.10), kind=kOutput, calls=%fused_computation.66 | convolution fusion | flops 18866700288 | bytes 74858496 | tf_op jit(solution)/shard_map/transpose(jvp())/dot_general | solution.py:22
  484.5 0.0 reduce-scatter.11.cloned.1.call-update
  484.5 0.0 reduce-scatter.13.cloned.1.call-start
  484.6 34.2 %fusion.32 = bf16[896,2560]{1,0:T(8,128)(2,1)} fusion(bf16[4096,2560]{1,0:T(8,128)(2,1)} %convolution_convert_fusion.1, bf16[4096,896]{0,1:T(8,128)(2,1)} %get-tuple-element.33, f32[4096]{0:T(1024)S(1)} %copy-done.6, f32[4096,2560]{1,0:T(8,128)} %get-tuple-element.35), kind=kOutput, calls=%fused_computation.64 | convolution fusion | flops 18866700288 | bytes 74858496 | tf_op jit(solution)/shard_map/transpose(jvp())/dot_general | solution.py:22
  518.8 0.0 reduce-scatter.7.cloned.1.call-start
  518.8 42.0 %fusion.33 = bf16[896,2560]{1,0:T(8,128)(2,1)} fusion(f32[4096,2560]{1,0:T(8,128)} %fusion.47, f32[4096,2560]{1,0:T(8,128)} %get-tuple-element.31, bf16[4096,2560]{1,0:T(8,128)(2,1)} %convolution_convert_fusion, bf16[1,4096,896]{1,2,0:T(8,128)(2,1)} %copy.20, f32[4096]{0:T(1024)S(1)} %copy-done.10), kind=kOutput, calls=%fused_computation.65 | convolution fusion | flops 18919129088 | bytes 116801536 | tf_op jit(solution)/shard_map/transpose(jvp())/dot_general | solution.py:21
  560.9 0.0 reduce-scatter.9.cloned.1.call-start
  560.9 25.3 %convolution_convert_fusion.3 = bf16[896,2560]{1,0:T(8,128)(2,1)} fusion(bf16[4096,2560]{1,0:T(8,128)(2,1)} %get-tuple-element.34, bf16[4096,896]{0,1:T(8,128)(2,1)} %get-tuple-element.33, f32[4096]{0:T(1024)S(1)} %copy-done.6), kind=kOutput, calls=%fused_computation.68 | convolution fusion | flops 18801491968 | bytes 32915456 | tf_op jit(solution)/shard_map/transpose(jvp())/dot_general | solution.py:21
  586.2 0.0 all-reduce.3.cloned.1.call-start
  586.3 0.0 reduce-scatter.15.cloned.1.call-done
  586.3 0.0 reduce-scatter.17.cloned.1.call-done
  586.4 0.0 reduce-scatter.11.cloned.1.call-done
  586.4 0.0 reduce-scatter.13.cloned.1.call-done
  586.4 26.6 %reduce-scatter.7.cloned.1.call-done = bf16[224,2560]{1,0:T(8,128)(2,1)} async-done(((bf16[896,2560]{1,0:T(8,128)(2,1)}), bf16[224,2560]{1,0:T(8,128)(2,1)}) %reduce-scatter.7.cloned.1.call-update) | async-done | bytes 1146896 | tf_op jit(solution)/shard_map/reduce_scatter | solution.py:43
  613.0 43.7 %reduce-scatter.9.cloned.1.call-done = bf16[224,2560]{1,0:T(8,128)(2,1)} async-done(((bf16[896,2560]{1,0:T(8,128)(2,1)}), bf16[224,2560]{1,0:T(8,128)(2,1)}) %reduce-scatter.9.cloned.1.call-update) | async-done | bytes 1146896 | tf_op jit(solution)/shard_map/reduce_scatter | solution.py:43
  656.7 163.2 %all-reduce.3.cloned.1.call-done = (bf16[1,224,2560]{2,1,0:T(8,128)(2,1)}, bf16[1,224,2560]{2,1,0:T(8,128)(2,1)}, bf16[1,224,2560]{2,1,0:T(8,128)(2,1)}, bf16[1,...) async-done(((bf16[1,224,2560]{2,1,0:T(8,128)(2,1)}, bf16[1,224,2560]{2,1,0:T(8,128)(2,1)}, bf16[1,224,2560]{2,1,0:T(8,128)(2,1)}, ...) | async-done | bytes 6881296 | tf_op jit(solution)/shard_map/psum | solution.py:43
  819.9 3.4 fusion.57
  823.3 3.4 fusion.56
  826.6 3.4 fusion.55
  832.0 6.8 psum.55
  839.5 9.5 %fusion.63 = (bf16[2,640,896]{2,1,0:T(8,128)(2,1)}, f32[2,640,896]{2,1,0:T(8,128)}, f32[2,640,896]{2,1,0:T(8,128)}) fusion(bf16[2,640,896]{2,1,0:T(8,128)(2,1)} %param.15, f32[]{:T(128)S(6)} %min_shard_map.3, bf16[1,640,896]{2,1,0:T(8,128)(2,1)} %get-tuple-element.13, bf16[1,640,896]{2,1,0:T(8,128)(2,1)} %get-tuple-element.14, f32[2,640,896]{2,1,0:T(8,128)} %param.21, ...), kind=kLoop, calls=%fused_computation.87 | loop fusion | flops 22937600 | bytes 25231364 | tf_op jit(solution)/shard_map/convert_element_type | solution.py:30
  849.0 14.6 %fusion.54 = (bf16[2,224,2560]{2,1,0:T(8,128)(2,1)}, f32[2,224,2560]{2,1,0:T(8,128)}, f32[2,224,2560]{2,1,0:T(8,128)}, bf16[2,224,2560]{2,1,0:T(8,128)(2,1)}, f3...) fusion(bf16[2,224,2560]{2,1,0:T(8,128)(2,1)S(1)} %copy-done, f32[]{:T(128)S(6)} %min_shard_map.3, ...), kind=kLoop, calls=%fused_computation.78 | loop fusion | flops 45875200 | bytes 50462724 | tf_op jit(solution)/shard_map/convert_element_type | solution.py:30
  (30 shorter events, 0.2 us)
Async XLA Ops:
  7.2 6.6 copy-start.2
  7.2 40.1 %all-gather.13.cloned.1.call-start = ((), (), s32[]{:S(2)}) async-start(), calls=%async_computation.12 | async-start | bytes 5734400 | tf_op jit(solution)/shard_map/all_gather | solution.py:40
  10.5 72.7 %all-gather.15.cloned.1.call-start = ((), (), s32[]{:S(2)}) async-start(), calls=%async_computation.13 | async-start | bytes 5734400 | tf_op jit(solution)/shard_map/all_gather | solution.py:40
  13.8 119.2 %all-gather.17.cloned.1.call-start = ((), (), s32[]{:S(2)}) async-start(), calls=%async_computation.14 | async-start | bytes 5734400 | tf_op jit(solution)/shard_map/all_gather | solution.py:40
  15.4 145.0 %all-gather.23.cloned.1.call-start = ((), (), s32[]{:S(2)}) async-start(), calls=%async_computation.17 | async-start | bytes 5734400 | tf_op jit(solution)/shard_map/all_gather | solution.py:40
  16.0 174.7 %all-gather.21.cloned.1.call-start = ((), (), s32[]{:S(2)}) async-start(), calls=%async_computation.16 | async-start | bytes 5734400 | tf_op jit(solution)/shard_map/all_gather | solution.py:40
  16.6 209.8 %all-gather.19.cloned.1.call-start = ((), (), s32[]{:S(2)}) async-start(), calls=%async_computation.15 | async-start | bytes 5734400 | tf_op jit(solution)/shard_map/all_gather | solution.py:40
  17.1 569.2 %reduce-scatter.15.cloned.1.call-start = ((), (), s32[]{:S(2)}) async-start(), calls=%async_computation.10 | async-start | bytes 5734400 | tf_op jit(solution)/shard_map/reduce_scatter | solution.py:43
  32.5 50.7 %copy-start.9 = (f32[4096]{0:T(1024)}, f32[4096]{0:T(1024)S(1)}, u32[]{:S(2)}) copy-start(f32[4096]{0:T(1024)S(1)} %add_rsqrt_fusion) | copy-start | bytes 49156
  159.7 0.6 copy-start.7
  160.4 186.7 %copy-start.5 = (f32[4096]{0:T(1024)}, f32[4096]{0:T(1024)S(1)}, u32[]{:S(2)}) copy-start(f32[4096]{0:T(1024)S(1)} %fusion.77) | copy-start | bytes 49156
  226.4 58.4 %copy-start.11 = (bf16[1,896,2560]{2,1,0:T(8,128)(2,1)S(1)}, bf16[1,896,2560]{2,1,0:T(8,128)(2,1)}, u32[]{:S(2)}) copy-start(bf16[1,896,2560]{2,1,0:T(8,128)(2,1)} %all-gather.19.cloned.1.call-done) | copy-start | bytes 13762564
  308.3 38.7 %copy-start.8 = (f32[4096]{0:T(1024)S(1)}, f32[4096]{0:T(1024)}, u32[]{:S(2)}) copy-start(f32[4096]{0:T(1024)} %copy-done.7) | copy-start | bytes 49156
  356.9 3.0 copy-start.3
  386.3 200.0 %reduce-scatter.17.cloned.1.call-start = ((), (), s32[]{:S(2)}) async-start(), calls=%async_computation.11 | async-start | bytes 5734400 | tf_op jit(solution)/shard_map/reduce_scatter | solution.py:43
  422.6 27.8 %copy-start.10 = (f32[4096]{0:T(1024)S(1)}, f32[4096]{0:T(1024)}, u32[]{:S(2)}) copy-start(f32[4096]{0:T(1024)} %copy-done.9) | copy-start | bytes 49156
  422.6 163.8 %reduce-scatter.11.cloned.1.call-start = ((), (), s32[]{:S(2)}) async-start(), calls=%async_computation.8 | async-start | bytes 5734400 | tf_op jit(solution)/shard_map/reduce_scatter | solution.py:43
  450.4 34.2 %copy-start.6 = (f32[4096]{0:T(1024)S(1)}, f32[4096]{0:T(1024)}, u32[]{:S(2)}) copy-start(f32[4096]{0:T(1024)} %copy-done.5) | copy-start | bytes 49156
  484.5 101.9 %reduce-scatter.13.cloned.1.call-start = ((), (), s32[]{:S(2)}) async-start(), calls=%async_computation.9 | async-start | bytes 5734400 | tf_op jit(solution)/shard_map/reduce_scatter | solution.py:43
  518.8 94.2 %reduce-scatter.7.cloned.1.call-start = ((), (), s32[]{:S(2)}) async-start(), calls=%async_computation.6 | async-start | bytes 5734400 | tf_op jit(solution)/shard_map/reduce_scatter | solution.py:43
  560.9 95.8 %reduce-scatter.9.cloned.1.call-start = ((), (), s32[]{:S(2)}) async-start(), calls=%async_computation.7 | async-start | bytes 5734400 | tf_op jit(solution)/shard_map/reduce_scatter | solution.py:43
  586.2 233.6 %all-reduce.3.cloned.1.call-start = ((), (), s32[]{:S(2)}) async-start(), calls=%async_computation.18 | async-start | bytes 13762560 | tf_op jit(solution)/shard_map/psum | solution.py:43
  839.5 9.5 %copy-start = (bf16[2,224,2560]{2,1,0:T(8,128)(2,1)S(1)}, bf16[2,224,2560]{2,1,0:T(8,128)(2,1)}, u32[]{:S(2)}) copy-start(bf16[2,224,2560]{2,1,0:T(8,128)(2,1)} %param.13) | copy-start | bytes 6881284
  839.5 9.5 %copy-start.1 = (bf16[2,224,2560]{2,1,0:T(8,128)(2,1)S(1)}, bf16[2,224,2560]{2,1,0:T(8,128)(2,1)}, u32[]{:S(2)}) copy-start(bf16[2,224,2560]{2,1,0:T(8,128)(2,1)} %param.14) | copy-start | bytes 6881284
  839.5 9.5 %copy-start.4 = (bf16[1,224,2560]{2,1,0:T(8,128)(2,1)S(1)}, bf16[1,224,2560]{2,1,0:T(8,128)(2,1)}, u32[]{:S(2)}) copy-start(bf16[1,224,2560]{2,1,0:T(8,128)(2,1)} %get-tuple-element.9) | copy-start | bytes 3440644
Sparse Core Ops, SparseCore 0:
  10.7 36.5 all-gather.12
  49.4 33.7 all-gather.14
  85.3 33.7 all-gather.16
  121.1 33.7 all-gather.22
  156.8 33.7 all-gather.20
  192.6 33.7 all-gather.18
  386.4 40.7 reduce-scatter.14
  430.3 40.7 reduce-scatter.16
  484.6 40.7 reduce-scatter.10
  528.3 40.7 reduce-scatter.12
  572.2 40.7 reduce-scatter.6
  615.9 40.7 reduce-scatter.8
  659.7 160.1 all-reduce.2
where the time goes:
time: 877 us; the launch traced here: 870 us
  matrix products  511 us (58%)
  waiting for transfers between devices  254 us (29%)
  other arithmetic  48.6 us (6%)
  local copies, waits for them, and re-layouts  33.1 us (4%)
  between operations  17 us (2%)
    dot_general x5, matrix products, layer(): up = jnp.dot(a, w['w_up'], preferred_element_type=jnp.float32)  186 us
    dot_general x5, matrix products, layer(): gate = jnp.dot(a, w['w_gate'], preferred_element_type=jnp.float32)  179 us
    psum x1, waiting for transfers between devices, summed(): lax.psum(lax.psum_scatter(term, 's', scatter_dimension=0, tiled=True), 'r')  163 us
    dot_general x5, matrix products, matmul(): jnp.dot(a, w, preferred_element_type=jnp.float32).astype(jnp.bfloat16)  146 us
    reduce_scatter x6, waiting for transfers between devices, summed(): lax.psum_scatter(term, 's', scatter_dimension=0, tiled=True)  70.4 us
    unnamed x26, local copies, waits for them, and re-layouts  25.1 us
    convert_element_type x2, other arithmetic, adamw(): return ((w - 0.02 * step).astype(jnp.bfloat16), m, v)  24.1 us
    all_gather x6, waiting for transfers between devices, fetched(): lax.all_gather(w[number], 's', axis=0, tiled=True)  18.5 us
  transfers between devices with their start and end apart: 13, of which 7 were waited for; matrix products, arithmetic and copies ran while one was open for 45% of the time, Pallas kernels for 0%

commit v1 on v0

v1 whole, which is shorter than its diff:
```python
import jax
import jax.numpy as jnp
from jax import lax
from jax.experimental import pallas as pl
from jax.experimental.pallas import tpu as pltpu
from jax.sharding import PartitionSpec as P

D, FF, T = 896, 2560, 4096
IN, OUT = D // 4, FF // 4
CHUNK = 2 * OUT
F32, BF = jnp.float32, jnp.bfloat16
GRANT = 66_000_000
ANY = pl.BlockSpec(memory_space=pl.ANY)


def nn(a, b):
    return lax.dot_general(a, b, (((1,), (0,)), ((), ())), preferred_element_type=F32)


def nt(a, b):
    return lax.dot_general(a, b, (((1,), (1,)), ((), ())), preferred_element_type=F32)


def place(s, me):
    other = s ^ me
    return (other >> 1) | ((other & 1) << 1)


def whole(shape):
    return pl.BlockSpec(shape, lambda *_: (0,) * len(shape), pipeline_mode=pl.Buffered(1))


def rows(bm, width):
    return pl.BlockSpec((bm, width), lambda i, *_: (i, 0))


def cols(height, bm):
    return pl.BlockSpec((height, bm), lambda i, *_: (0, i))


def params():
    return pltpu.CompilerParams(vmem_limit_bytes=GRANT)


def scaled(h):
    wide = h.astype(F32)
    return wide, lax.rsqrt(jnp.mean(wide * wide, -1, keepdims=True) + 1e-6)


def put_rows(me, ref, value):
    for s in range(4):
        at = pl.multiple_of(place(s, me) * IN, 32)
        ref[pl.ds(at, IN), :] = value[s * IN : (s + 1) * IN, :]


def put_columns(me, ref, value, first):
    for k in range(value.shape[1] // OUT):
        at = pl.multiple_of(place(first + k, me) * OUT, 128)
        ref[:, pl.ds(at, OUT)] = value[:, k * OUT : (k + 1) * OUT]


def load_in(layer, me, r, own, got, buf, sem):
    core, x, y, core_x, core_y = got
    at = lambda s: pl.ds(pl.multiple_of(s * IN, 32), IN)
    return [
        pltpu.make_async_copy(own[0].at[layer], buf.at[0, at(me)], sem.at[0]),
        pltpu.make_async_copy(own[1].at[layer], buf.at[1, at(me)], sem.at[1]),
        pltpu.make_async_copy(core, buf.at[:, at(me ^ 1)], sem.at[2]),
        pltpu.make_async_copy(x, buf.at[r, at(me ^ 2)], sem.at[3]),
        pltpu.make_async_copy(y, buf.at[1 - r, at(me ^ 2)], sem.at[4]),
        pltpu.make_async_copy(core_x, buf.at[r, at(me ^ 3)], sem.at[5]),
        pltpu.make_async_copy(core_y, buf.at[1 - r, at(me ^ 3)], sem.at[6]),
    ]


def load_down(layer, r, own, got, buf, sem):
    core, x, y, core_x, core_y = got
    half = OUT // 2
    at = lambda block, which: pl.ds(pl.multiple_of(block * OUT + which * half, 32), half)
    return [
        pltpu.make_async_copy(own.at[layer], buf.at[pl.ds(0, OUT)], sem.at[0]),
        pltpu.make_async_copy(core, buf.at[pl.ds(2 * OUT, OUT)], sem.at[1]),
        pltpu.make_async_copy(x, buf.at[at(1, r)], sem.at[2]),
        pltpu.make_async_copy(y, buf.at[at(1, 1 - r)], sem.at[3]),
        pltpu.make_async_copy(core_x, buf.at[at(3, r)], sem.at[4]),
        pltpu.make_async_copy(core_y, buf.at[at(3, 1 - r)], sem.at[5]),
    ]


SCRATCH = [
    pltpu.VMEM((2, D, FF), BF),
    pltpu.VMEM((FF, D), BF),
    pltpu.SemaphoreType.DMA((7,)),
    pltpu.SemaphoreType.DMA((6,)),
]


def load(where, in_layer, down_layer, refs, scratch):
    own, got_in, got_down = refs[:3], refs[3:8], refs[8:13]
    w_in, w_down, in_sem, down_sem = scratch
    me, r = where[0], where[1]

    @pl.when(pl.program_id(0) == 0)
    def _():
        first = load_in(in_layer, me, r, own, got_in, w_in, in_sem)
        second = load_down(down_layer, r, own[2], got_down, w_down, down_sem)
        for copy in first + second:
            copy.start()
        for copy in first + second:
            copy.wait()


def down_rows(me, w_down, block):
    return w_down[pl.ds(pl.multiple_of(place(block, me) * OUT, OUT), OUT), :]


def first_kernel(where, x_ref, *refs):
    weights, (act_ref, gate_ref, up_ref, h_ref, at_ref), scratch = refs[:13], refs[13:18], refs[18:]
    w_in, w_down = scratch[:2]
    me = where[0]
    load(where, 0, 0, weights, scratch)
    x = x_ref[...]
    wide, scale = scaled(x)
    a = (wide * scale).astype(BF)
    put_rows(me, at_ref, a.T)
    for n in range(0, FF, CHUNK):
        gate = nn(a, w_in[0, :, n : n + CHUNK])
        up = nn(a, w_in[1, :, n : n + CHUNK])
        gate_ref[:, n : n + CHUNK] = gate
        up_ref[:, n : n + CHUNK] = up
        put_columns(me, act_ref, (gate * jax.nn.sigmoid(gate) * up).astype(BF), n // OUT)
    h_ref[...] = x + nn(act_ref[...], w_down[...]).astype(BF)


def first_layer(where, x, weights, bm=512):
    return pl.pallas_call(
        first_kernel,
        grid_spec=pltpu.PrefetchScalarGridSpec(
            num_scalar_prefetch=1,
            grid=(T // bm,),
            in_specs=[rows(bm, D)] + [ANY] * 13,
            out_specs=[rows(bm, FF), rows(bm, FF), rows(bm, FF), rows(bm, D), cols(D, bm)],
            scratch_shapes=SCRATCH,
        ),
        out_shape=[jax.ShapeDtypeStruct((T, FF), dtype) for dtype in (BF, F32, F32)]
        + [jax.ShapeDtypeStruct((T, D), BF), jax.ShapeDtypeStruct((D, T), BF)],
        compiler_params=params(),
        cost_estimate=pl.CostEstimate(flops=6 * T * D * FF, bytes_accessed=140 << 20, transcendentals=0),
        name="first_layer",
    )(where, x, *weights)


def back_through_act(dact, gate, up):
    sig = jax.nn.sigmoid(gate)
    silu = gate * sig
    return silu, (dact * up * (sig * (1.0 + gate - silu))).astype(BF), (dact * silu).astype(BF)


def dact_of(me, dh, w_down, n):
    parts = [nt(dh, down_rows(me, w_down, n // OUT + k)) for k in range(CHUNK // OUT)]
    return jnp.concatenate(parts, axis=1).astype(BF).astype(F32)


def second_kernel(where, h_ref, dy_ref, *refs):
    weights, (act_ref, dgate_ref, dup_ref, at_ref, dyt_ref), scratch = refs[:13], refs[13:18], refs[18:]
    w_in, w_down = scratch[:2]
    me = where[0]
    load(where, 1, 1, weights, scratch)
    wide, scale = scaled(h_ref[...])
    a = (wide * scale).astype(BF)
    put_rows(me, at_ref, a.T)
    dy = dy_ref[...]
    dyt_ref[...] = dy.T
    for n in range(0, FF, CHUNK):
        gate = nn(a, w_in[0, :, n : n + CHUNK])
        up = nn(a, w_in[1, :, n : n + CHUNK])
        silu, dgate, dup = back_through_act(dact_of(me, dy, w_down, n), gate, up)
        put_columns(me, act_ref, (silu * up).astype(BF), n // OUT)
        dgate_ref[:, n : n + CHUNK] = dgate
        dup_ref[:, n : n + CHUNK] = dup


def second_layer(where, h, dy, weights, bm=256):
    return pl.pallas_call(
        second_kernel,
        grid_spec=pltpu.PrefetchScalarGridSpec(
            num_scalar_prefetch=1,
            grid=(T // bm,),
            in_specs=[rows(bm, D), rows(bm, D)] + [ANY] * 13,
            out_specs=[rows(bm, FF)] * 3 + [cols(D, bm)] * 2,
            scratch_shapes=SCRATCH,
        ),
        out_shape=[jax.ShapeDtypeStruct((T, FF), BF)] * 3 + [jax.ShapeDtypeStruct((D, T), BF)] * 2,
        compiler_params=params(),
        cost_estimate=pl.CostEstimate(flops=6 * T * D * FF, bytes_accessed=100 << 20, transcendentals=0),
        name="second_layer",
    )(where, h, dy, *weights)


def between_kernel(where, h_ref, dy_ref, dgate1_ref, dup1_ref, gate_ref, up_ref, *refs):
    weights, (dgate_ref, dup_ref, dht_ref), scratch = refs[:13], refs[13:16], refs[16:]
    w_in, w_down = scratch[:2]
    me = where[0]
    load(where, 1, 0, weights, scratch)
    da = nt(dgate1_ref[...], w_in[0]).astype(BF).astype(F32) + nt(dup1_ref[...], w_in[1]).astype(BF).astype(F32)
    da = da.astype(BF).astype(F32)
    wide, scale = scaled(h_ref[...])
    through = da * scale - wide * (scale * scale * scale * jnp.mean(da * wide, -1, keepdims=True))
    dh = dy_ref[...] + through.astype(BF)
    dht_ref[...] = dh.T
    for n in range(0, FF, CHUNK):
        gate, up = gate_ref[:, n : n + CHUNK], up_ref[:, n : n + CHUNK]
        _, dgate, dup = back_through_act(dact_of(me, dh, w_down, n), gate, up)
        dgate_ref[:, n : n + CHUNK] = dgate
        dup_ref[:, n : n + CHUNK] = dup


def between_layers(where, h, dy, dgate1, dup1, gate, up, weights, bm=256):
    return pl.pallas_call(
        between_kernel,
        grid_spec=pltpu.PrefetchScalarGridSpec(
            num_scalar_prefetch=1,
            grid=(T // bm,),
            in_specs=[rows(bm, D), rows(bm, D)] + [rows(bm, FF)] * 4 + [ANY] * 13,
            out_specs=[rows(bm, FF), rows(bm, FF), cols(D, bm)],
            scratch_shapes=SCRATCH,
        ),
        out_shape=[jax.ShapeDtypeStruct((T, FF), BF)] * 2 + [jax.ShapeDtypeStruct((D, T), BF)],
        compiler_params=params(),
        cost_estimate=pl.CostEstimate(flops=6 * T * D * FF, bytes_accessed=180 << 20, transcendentals=0),
        name="between_layers",
    )(where, h, dy, dgate1, dup1, gate, up, *weights)


def by_in_kernel(left, right, mine_ref, theirs_ref):
    out = nn(left[...], right[...]).astype(BF)
    mine_ref[...] = out[: 2 * IN]
    theirs_ref[...] = out[2 * IN :]


def by_in(at, d, first, width, bn=256):
    tile = pl.BlockSpec((2 * IN, bn), lambda j: (0, j))
    return pl.pallas_call(
        by_in_kernel,
        grid=(width // bn,),
        in_specs=[whole((D, T)), pl.BlockSpec((T, bn), lambda j: (0, j + first // bn))],
        out_specs=[tile, tile],
        out_shape=[jax.ShapeDtypeStruct((2 * IN, width), BF)] * 2,
        compiler_params=params(),
        cost_estimate=pl.CostEstimate(flops=2 * T * D * width, bytes_accessed=40 << 20, transcendentals=0),
        name="by_in",
    )(at, d)


def by_down_kernel(left, right, out_ref):
    out_ref[...] = nn(left[...], right[...]).T.astype(BF)


def by_down(dht, act, first, width, bn=256):
    return pl.pallas_call(
        by_down_kernel,
        grid=(width // bn,),
        in_specs=[whole((D, T)), pl.BlockSpec((T, bn), lambda j: (0, j + first // bn))],
        out_specs=pl.BlockSpec((bn, D), lambda j: (j, 0)),
        out_shape=jax.ShapeDtypeStruct((width, D), BF),
        compiler_params=params(),
        cost_estimate=pl.CostEstimate(flops=2 * T * D * width, bytes_accessed=40 << 20, transcendentals=0),
        name="by_down",
    )(dht, act)


def core(value):
    return lax.ppermute(value, "s", [(i, i ^ 1) for i in range(4)])


def along_x(value):
    return lax.ppermute(value, "s", [(i, i ^ 2) for i in range(4)])


def along_y(value):
    return lax.ppermute(value, "r", [(0, 1), (1, 0)])


def pieces(block, half):
    x = along_x(half)
    y = along_y(x)
    return core(block), x, y, core(x), core(y)


def term(mine, theirs):
    got = core(theirs)
    height = mine.shape[0] // 2
    add = lambda a, b: a.astype(F32) + b.astype(F32)
    x = along_x(add(mine[height:], got[height:]).astype(BF))
    total = (add(mine[:height], got[:height]) + x.astype(F32)).astype(BF)
    return total, along_y(total)


def adamw(w, m, v, g):
    m = 0.9 * m + 0.1 * g
    v = 0.95 * v + 0.05 * g * g
    step = m * lax.rsqrt(v + 1e-8) + 0.1 * w
    return (w - 0.02 * step).astype(jnp.bfloat16), m, v


def clipped(gradients, sum_of_squares, count):
    factor = jnp.minimum(1.0, 0.5 * lax.rsqrt(sum_of_squares / count + 1e-30))
    return [g * factor for g in gradients]


def solution(mesh):
    def step(x, dy, *arrays):
        weights, m, v = (arrays[i : i + 3] for i in (0, 3, 6))
        x, dy = x[0], dy[0]
        me, r = lax.axis_index("s").astype(jnp.int32), lax.axis_index("r").astype(jnp.int32)
        where = jnp.stack([me, r])

        got_in, got_down = [], []
        for layer in range(2):
            both = jnp.stack([weights[0][layer], weights[1][layer]])
            got_in.append(pieces(both, lax.dynamic_index_in_dim(both, r, 0, keepdims=False)))
            block = weights[2][layer]
            got_down.append(pieces(block, lax.dynamic_slice_in_dim(block, r * (OUT // 2), OUT // 2, 0)))
        fetched = lambda i, j: (*weights, *got_in[i], *got_down[j])

        act0, gate0, up0, h, at0 = first_layer(where, x, fetched(0, 0))
        act1, dgate1, dup1, at1, dyt = second_layer(where, h, dy, fetched(1, 1))

        def down(dht, act):
            theirs = by_down(dht, act, 2 * OUT, 2 * OUT)
            return [term(by_down(dht, act, 0, 2 * OUT), theirs)]

        def inner(at, d, parts):
            width = FF // parts
            return [term(*by_in(at, d, i * width, width)) for i in range(parts)]

        down1 = down(dyt, act1)
        gate1, up1 = inner(at1, dgate1, 1), inner(at1, dup1, 1)
        dgate0, dup0, dht = between_layers(where, h, dy, dgate1, dup1, gate0, up0, fetched(1, 0))
        down0 = down(dht, act0)
        gate0, up0 = inner(at0, dgate0, 2), inner(at0, dup0, 2)

        def summed(parts, axis):
            return jnp.concatenate([(a.astype(F32) + b.astype(F32)).astype(BF) for a, b in parts], axis=axis)

        gradients = [
            jnp.stack([summed(first, axis), summed(second, axis)]).astype(F32)
            for first, second, axis in ((gate0, gate1, 1), (up0, up1, 1), (down0, down1, 0))
        ]
        squares = lax.psum(sum(jnp.sum(g * g) for g in gradients), "s")
        gradients = clipped(gradients, squares, lax.psum(1, "s") * sum(g.size for g in gradients))
        new = [adamw(w.astype(F32), m, v, g) for w, m, v, g in zip(weights, m, v, gradients, strict=True)]
        return tuple(one[which] for which in range(3) for one in new)

    states, cut = P(("rep", "r", "s"), None, None), P(None, "s", None)
    return jax.shard_map(
        step,
        mesh=mesh,
        in_specs=(states, states) + (cut,) * 9,
        out_specs=(P("rep", "s", None),) * 9,
        check_vma=False,
    )
```

time: 877 us -> 829 us (0.945)
  matrix products: 511 us -> 0 us
  Pallas kernels: 0 us -> 431 us
  starting transfers between devices: 0.53 us -> 38.2 us
  waiting for transfers between devices: 254 us -> 288 us
  local copies, waits for them, and re-layouts: 33.1 us -> 11 us
  between operations: 17 us -> 4.14 us
    dot_general x15 -> x0, matrix products: 511 us -> none  [the longest x5 186 us: layer(): up = jnp.dot(a, w['w_up'], preferred_element_type=jnp.float32)]
    pallas_call x0 -> x13, Pallas kernels: none -> 431 us  [the longest x6 110 us: by_in(): pl.pallas_call(by_in_kernel, grid=(width // bn,), in_specs=[whole((D, T))...]
    ppermute x0 -> x44, waiting for transfers between devices: none -> 288 us  [the longest x12 151 us: along_x(): return lax.ppermute(value, 's', [(i, i ^ 2) for i in range(4)])]
    psum x1 -> x0, waiting for transfers between devices: 163 us -> none  [summed(): lax.psum(lax.psum_scatter(term, 's', scatter_dimension=0, tiled=True), 'r')]
    reduce_scatter x6 -> x0, waiting for transfers between devices: 70.4 us -> none  [summed(): lax.psum_scatter(term, 's', scatter_dimension=0, tiled=True)]
    ppermute x0 -> x44, starting transfers between devices: none -> 38.2 us  [the longest x12 17.4 us: along_x(): return lax.ppermute(value, 's', [(i, i ^ 2) for i in range(4)])]
    unnamed x26 -> x60, local copies, waits for them, and re-layouts: 25.1 us -> 3.2 us
    all_gather x6 -> x0, waiting for transfers between devices: 18.5 us -> none  [fetched(): lax.all_gather(w[number], 's', axis=0, tiled=True)]
  transfers between devices with their start and end apart: 13 -> 44, of which waited for: 7 -> 18; matrix products, arithmetic and copies ran while one was open for 45% -> 3% of each run, Pallas kernels for 0% -> 13%
where the time goes in v1:
time: 829 us; the launch traced here: 826 us
  Pallas kernels  431 us (52%)
  waiting for transfers between devices  288 us (35%)
  other arithmetic  48.3 us (6%)
  starting transfers between devices  38.2 us (5%)
  local copies, waits for them, and re-layouts  11 us (1%)
    ppermute x12, waiting for transfers between devices, along_x(): return lax.ppermute(value, 's', [(i, i ^ 2) for i in range(4)])  151 us
    ppermute x12, waiting for transfers between devices, along_y(): return lax.ppermute(value, 'r', [(0, 1), (1, 0)])  132 us
    pallas_call x6, Pallas kernels, by_in(): pl.pallas_call(by_in_kernel, grid=(width // bn,), in_specs=[whole((D, T))...  110 us
    pallas_call x1, Pallas kernels, between_layers(): pl.pallas_call(between_kernel, grid_spec=pltpu.PrefetchScalarGridSpec(num...  93.8 us
    pallas_call x1, Pallas kernels, second_layer(): pl.pallas_call(second_kernel, grid_spec=pltpu.PrefetchScalarGridSpec(num_...  84.9 us
    pallas_call x1, Pallas kernels, first_layer(): pl.pallas_call(first_kernel, grid_spec=pltpu.PrefetchScalarGridSpec(num_s...  80.7 us
    pallas_call x4, Pallas kernels, by_down(): pl.pallas_call(by_down_kernel, grid=(width // bn,), in_specs=[whole((D, T...  61 us
    convert_element_type x3, other arithmetic, adamw(): return ((w - 0.02 * step).astype(jnp.bfloat16), m, v)  24.3 us
  transfers between devices with their start and end apart: 44, of which 18 were waited for; matrix products, arithmetic and copies ran while one was open for 3% of the time, Pallas kernels for 13%

profile of v1, /device:TPU:0, one launch (start us, length us, event | category | flops | bytes accessed | tf_op | source)
XLA Modules:
  0.0 826.3 jit_solution(7565160136964999599)
XLA Ops:
  0.6 2.6 fusion.36
  4.3 1.4 fusion.28
  5.7 3.3 collective-permute-start.1
  9.0 3.9 fusion.35
  14.6 2.0 collective-permute-start.11
  16.7 30.7 %collective-permute-done.6.refs_9_ = bf16[320,896]{1,0:T(8,128)(2,1)S(1)} collective-permute-done((bf16[320,896]{1,0:T(8,128)(2,1)S(1)}, bf16[320,896]{1,0:T(8,128)(2,1)S(1)}, u32[]{:S(2)}, u32[]{:S(2)}) %collective-permute-start.6) | collective-permute-done | bytes 573472 | tf_op jit(solution)/shard_map/ppermute | solution.py:277
  47.4 2.1 collective-permute-start.7
  49.5 1.6 pad_maximum_fusion
  51.1 32.4 %collective-permute-done.16.refs_9_ = bf16[320,896]{1,0:T(8,128)(2,1)S(1)} collective-permute-done((bf16[320,896]{1,0:T(8,128)(2,1)S(1)}, bf16[320,896]{1,0:T(8,128)(2,1)S(1)}, u32[]{:S(2)}, u32[]{:S(2)}) %collective-permute-start.16) | collective-permute-done | bytes 573472 | tf_op jit(solution)/shard_map/ppermute | solution.py:277
  83.4 1.8 collective-permute-start.2
  86.0 4.3 collective-permute-done.18.refs_11_
  90.5 33.0 %collective-permute-done.17.refs_10_ = bf16[320,896]{1,0:T(8,128)(2,1)} collective-permute-done((bf16[320,896]{1,0:T(8,128)(2,1)S(1)}, bf16[320,896]{1,0:T(8,128)(2,1)}, u32[]{:S(2)}, u32[]{:S(2)}) %collective-permute-start.17) | collective-permute-done | bytes 573472 | tf_op jit(solution)/shard_map/ppermute | solution.py:281
  123.4 1.7 collective-permute-start.12
  127.4 1.6 pad_maximum_fusion.1
  129.5 20.9 %collective-permute-done.12.refs_5_ = bf16[224,2560]{1,0:T(8,128)(2,1)} collective-permute-done((bf16[224,2560]{1,0:T(8,128)(2,1)}, bf16[224,2560]{1,0:T(8,128)(2,1)}, u32[]{:S(2)}, u32[]{:S(2)}) %collective-permute-start.12) | collective-permute-done | bytes 1146912 | tf_op jit(solution)/shard_map/ppermute | solution.py:281
  150.9 80.7 %first_layer.1 = (bf16[4096,2560]{1,0:T(8,128)(2,1)}, f32[4096,2560]{1,0:T(8,128)}, f32[4096,2560]{1,0:T(8,128)}, bf16[4096,896]{1,0:T(8,128)(2,1)}, bf16[896,4096]{1,0:T(8,128)(2,1)}) custom-call(s32[2]{0:T(128)} %pad_add_fusion.where, bf16[4096,896]{1,0:T(8,128)(2,1)} %bitcast.32, bf16[2,224,2560]{2,1,0:T(8,128)(2,1)} %refs_0_.5, ...), custom_call_target="tpu_custom_call" | custom-call | flops 56371445760 | bytes 146800640 | tf_op jit(solution)/shard_map/first_layer/pallas_call | solution.py:136
  231.6 84.9 %second_layer.1 = (bf16[4096,2560]{1,0:T(8,128)(2,1)}, bf16[4096,2560]{1,0:T(8,128)(2,1)}, bf16[4096,2560]{1,0:T(8,128)(2,1)}, bf16[896,4096]{1,0:T(8,128)(2,1)}, bf16[896,4096]{1,0:T(8,128)(2,1)}) custom-call(s32[2]{0:T(128)} %pad_add_fusion.where, bf16[4096,896]{1,0:T(8,128)(2,1)} %get-tuple-element.35.h_ref, bf16[4096,896]{1,0:T(8,128)(2,1)} %bitcast.33, ...), custom_call_target="tpu_custom_call" | custom-call | flops 56371445760 | bytes 104857600 | tf_op jit(solution)/shard_map/second_layer/pallas_call | solution.py:184
  316.6 25.2 %by_in.11 = (bf16[448,2560]{1,0:T(8,128)(2,1)}, bf16[448,2560]{1,0:T(8,128)(2,1)}) custom-call(bf16[896,4096]{1,0:T(8,128)(2,1)} %get-tuple-element.45.left, bf16[4096,2560]{1,0:T(8,128)(2,1)} %get-tuple-element.37.dup1_ref.right), custom_call_target="tpu_custom_call" | custom-call | flops 18790481920 | bytes 41943040 | tf_op jit(solution)/shard_map/by_in/pallas_call | solution.py:243
  341.8 25.4 %by_in.8 = (bf16[448,2560]{1,0:T(8,128)(2,1)}, bf16[448,2560]{1,0:T(8,128)(2,1)}) custom-call(bf16[896,4096]{1,0:T(8,128)(2,1)} %get-tuple-element.45.left, bf16[4096,2560]{1,0:T(8,128)(2,1)} %get-tuple-element.36.dgate1_ref.right), custom_call_target="tpu_custom_call" | custom-call | flops 18790481920 | bytes 41943040 | tf_op jit(solution)/shard_map/by_in/pallas_call | solution.py:243
  367.1 93.8 %between_layers.1 = (bf16[4096,2560]{1,0:T(8,128)(2,1)}, bf16[4096,2560]{1,0:T(8,128)(2,1)}, bf16[896,4096]{1,0:T(8,128)(2,1)}) custom-call(s32[2]{0:T(128)} %pad_add_fusion.where, bf16[4096,896]{1,0:T(8,128)(2,1)} %get-tuple-element.35.h_ref, bf16[4096,896]{1,0:T(8,128)(2,1)} %bitcast.34, bf16[4096,2560]{1,0:T(8,128)(2,1)} %get-tuple-element.36.dgate1_ref.right, ...), custom_call_target="tpu_custom_call" | custom-call | flops 56371445760 | bytes 188743680 | tf_op jit(solution)/shard_map/between_layers/pallas_call | solution.py:219
  461.0 15.2 %by_down.4 = bf16[1280,896]{1,0:T(8,128)(2,1)} custom-call(bf16[896,4096]{1,0:T(8,128)(2,1)} %get-tuple-element.55.left, bf16[4096,2560]{1,0:T(8,128)(2,1)} %get-tuple-element.56.right), custom_call_target="tpu_custom_call" | custom-call | flops 9395240960 | bytes 41943040 | tf_op jit(solution)/shard_map/by_down/pallas_call | solution.py:260
  476.2 15.2 %by_down.5 = bf16[1280,896]{1,0:T(8,128)(2,1)} custom-call(bf16[896,4096]{1,0:T(8,128)(2,1)} %get-tuple-element.55.left, bf16[4096,2560]{1,0:T(8,128)(2,1)} %get-tuple-element.56.right), custom_call_target="tpu_custom_call" | custom-call | flops 9395240960 | bytes 41943040 | tf_op jit(solution)/shard_map/by_down/pallas_call | solution.py:260
  491.5 15.2 %by_down.6 = bf16[1280,896]{1,0:T(8,128)(2,1)} custom-call(bf16[896,4096]{1,0:T(8,128)(2,1)} %get-tuple-element.57.left, bf16[4096,2560]{1,0:T(8,128)(2,1)} %get-tuple-element.58.right), custom_call_target="tpu_custom_call" | custom-call | flops 9395240960 | bytes 41943040 | tf_op jit(solution)/shard_map/by_down/pallas_call | solution.py:260
  506.7 15.2 %by_down.7 = bf16[1280,896]{1,0:T(8,128)(2,1)} custom-call(bf16[896,4096]{1,0:T(8,128)(2,1)} %get-tuple-element.57.left, bf16[4096,2560]{1,0:T(8,128)(2,1)} %get-tuple-element.58.right), custom_call_target="tpu_custom_call" | custom-call | flops 9395240960 | bytes 41943040 | tf_op jit(solution)/shard_map/by_down/pallas_call | solution.py:260
  521.9 15.1 %by_in.7 = (bf16[448,1280]{1,0:T(8,128)(2,1)}, bf16[448,1280]{1,0:T(8,128)(2,1)}) custom-call(bf16[896,4096]{1,0:T(8,128)(2,1)} %get-tuple-element.34.left, bf16[4096,2560]{1,0:T(8,128)(2,1)} %get-tuple-element.40.right), custom_call_target="tpu_custom_call" | custom-call | flops 9395240960 | bytes 41943040 | tf_op jit(solution)/shard_map/by_in/pallas_call | solution.py:243
  537.0 14.8 %by_in.6 = (bf16[448,1280]{1,0:T(8,128)(2,1)}, bf16[448,1280]{1,0:T(8,128)(2,1)}) custom-call(bf16[896,4096]{1,0:T(8,128)(2,1)} %get-tuple-element.34.left, bf16[4096,2560]{1,0:T(8,128)(2,1)} %get-tuple-element.40.right), custom_call_target="tpu_custom_call" | custom-call | flops 9395240960 | bytes 41943040 | tf_op jit(solution)/shard_map/by_in/pallas_call | solution.py:243
  552.4 14.9 %by_in.10 = (bf16[448,1280]{1,0:T(8,128)(2,1)}, bf16[448,1280]{1,0:T(8,128)(2,1)}) custom-call(bf16[896,4096]{1,0:T(8,128)(2,1)} %get-tuple-element.34.left, bf16[4096,2560]{1,0:T(8,128)(2,1)} %get-tuple-element.48.right), custom_call_target="tpu_custom_call" | custom-call | flops 9395240960 | bytes 41943040 | tf_op jit(solution)/shard_map/by_in/pallas_call | solution.py:243
  567.6 14.9 %by_in.9 = (bf16[448,1280]{1,0:T(8,128)(2,1)}, bf16[448,1280]{1,0:T(8,128)(2,1)}) custom-call(bf16[896,4096]{1,0:T(8,128)(2,1)} %get-tuple-element.34.left, bf16[4096,2560]{1,0:T(8,128)(2,1)} %get-tuple-element.48.right), custom_call_target="tpu_custom_call" | custom-call | flops 9395240960 | bytes 41943040 | tf_op jit(solution)/shard_map/by_in/pallas_call | solution.py:243
  583.1 1.5 add_convert_fusion.20
  585.0 1.5 add_convert_fusion.23
  586.5 1.7 collective-permute-start.24
  590.0 12.4 %collective-permute-done.24 = bf16[224,1280]{1,0:T(8,128)(2,1)S(1)} collective-permute-done((bf16[224,1280]{1,0:T(8,128)(2,1)S(1)}, bf16[224,1280]{1,0:T(8,128)(2,1)S(1)}, u32[]{:S(2)}, u32[]{:S(2)}) %collective-permute-start.24) | collective-permute-done | bytes 573472 | tf_op jit(solution)/shard_map/ppermute | solution.py:277
  602.4 1.7 collective-permute-start.33
  605.4 9.3 %collective-permute-done.21 = bf16[224,1280]{1,0:T(8,128)(2,1)S(1)} collective-permute-done((bf16[224,1280]{1,0:T(8,128)(2,1)S(1)}, bf16[224,1280]{1,0:T(8,128)(2,1)S(1)}, u32[]{:S(2)}, u32[]{:S(2)}) %collective-permute-start.21) | collective-permute-done | bytes 573472 | tf_op jit(solution)/shard_map/ppermute | solution.py:277
  614.7 1.7 collective-permute-start.30
  616.4 1.3 add_convert_fusion.22
  617.7 9.3 %collective-permute-done.33 = bf16[224,1280]{1,0:T(8,128)(2,1)S(1)} collective-permute-done((bf16[224,1280]{1,0:T(8,128)(2,1)S(1)}, bf16[224,1280]{1,0:T(8,128)(2,1)S(1)}, u32[]{:S(2)}, u32[]{:S(2)}) %collective-permute-start.33) | collective-permute-done | bytes 573472 | tf_op jit(solution)/shard_map/ppermute | solution.py:277
  628.2 10.1 %collective-permute-done.30 = bf16[224,1280]{1,0:T(8,128)(2,1)S(1)} collective-permute-done((bf16[224,1280]{1,0:T(8,128)(2,1)S(1)}, bf16[224,1280]{1,0:T(8,128)(2,1)S(1)}, u32[]{:S(2)}, u32[]{:S(2)}) %collective-permute-start.30) | collective-permute-done | bytes 573472 | tf_op jit(solution)/shard_map/ppermute | solution.py:277
  638.4 1.7 collective-permute-start.25
  641.0 1.7 collective-permute-start.34
  643.7 1.6 collective-permute-start.42
  645.6 8.6 %collective-permute-done.25 = bf16[224,1280]{1,0:T(8,128)(2,1)S(1)} collective-permute-done((bf16[224,1280]{1,0:T(8,128)(2,1)S(1)}, bf16[224,1280]{1,0:T(8,128)(2,1)S(1)}, u32[]{:S(2)}, u32[]{:S(2)}) %collective-permute-start.25) | collective-permute-done | bytes 573472 | tf_op jit(solution)/shard_map/ppermute | solution.py:281
  654.2 1.6 collective-permute-start.39
  656.0 10.5 %collective-permute-done.22 = bf16[224,1280]{1,0:T(8,128)(2,1)S(1)} collective-permute-done((bf16[224,1280]{1,0:T(8,128)(2,1)S(1)}, bf16[224,1280]{1,0:T(8,128)(2,1)S(1)}, u32[]{:S(2)}, u32[]{:S(2)}) %collective-permute-start.22) | collective-permute-done | bytes 573472 | tf_op jit(solution)/shard_map/ppermute | solution.py:281
  666.5 1.6 collective-permute-start.36
  668.3 10.5 %collective-permute-done.34 = bf16[224,1280]{1,0:T(8,128)(2,1)S(1)} collective-permute-done((bf16[224,1280]{1,0:T(8,128)(2,1)S(1)}, bf16[224,1280]{1,0:T(8,128)(2,1)S(1)}, u32[]{:S(2)}, u32[]{:S(2)}) %collective-permute-start.34) | collective-permute-done | bytes 573472 | tf_op jit(solution)/shard_map/ppermute | solution.py:281
  678.8 1.6 collective-permute-start.27
  680.6 8.8 %collective-permute-done.31 = bf16[224,1280]{1,0:T(8,128)(2,1)S(1)} collective-permute-done((bf16[224,1280]{1,0:T(8,128)(2,1)S(1)}, bf16[224,1280]{1,0:T(8,128)(2,1)S(1)}, u32[]{:S(2)}, u32[]{:S(2)}) %collective-permute-start.31) | collective-permute-done | bytes 573472 | tf_op jit(solution)/shard_map/ppermute | solution.py:281
  690.1 1.7 collective-permute-start.43
  691.9 4.5 collective-permute-done.39
  696.8 1.7 collective-permute-start.40
  698.6 22.4 %collective-permute-done.36 = bf16[224,2560]{1,0:T(8,128)(2,1)S(1)} collective-permute-done((bf16[224,2560]{1,0:T(8,128)(2,1)S(1)}, bf16[224,2560]{1,0:T(8,128)(2,1)S(1)}, u32[]{:S(2)}, u32[]{:S(2)}) %collective-permute-start.36) | collective-permute-done | bytes 1146912 | tf_op jit(solution)/shard_map/ppermute | solution.py:277
  721.4 1.7 collective-permute-start.37
  723.1 19.8 %collective-permute-done.27 = bf16[224,2560]{1,0:T(8,128)(2,1)S(1)} collective-permute-done((bf16[224,2560]{1,0:T(8,128)(2,1)S(1)}, bf16[224,2560]{1,0:T(8,128)(2,1)S(1)}, u32[]{:S(2)}, u32[]{:S(2)}) %collective-permute-start.27) | collective-permute-done | bytes 1146912 | tf_op jit(solution)/shard_map/ppermute | solution.py:277
  743.4 1.5 collective-permute-start.28
  745.5 1.8 fusion.11
  747.2 20.2 %collective-permute-done.37 = bf16[224,2560]{1,0:T(8,128)(2,1)S(1)} collective-permute-done((bf16[224,2560]{1,0:T(8,128)(2,1)S(1)}, bf16[224,2560]{1,0:T(8,128)(2,1)S(1)}, u32[]{:S(2)}, u32[]{:S(2)}) %collective-permute-start.37) | collective-permute-done | bytes 1146912 | tf_op jit(solution)/shard_map/ppermute | solution.py:281
  767.7 1.8 fusion.10
  769.5 19.9 %collective-permute-done.28 = bf16[224,2560]{1,0:T(8,128)(2,1)S(1)} collective-permute-done((bf16[224,2560]{1,0:T(8,128)(2,1)S(1)}, bf16[224,2560]{1,0:T(8,128)(2,1)S(1)}, u32[]{:S(2)}, u32[]{:S(2)}) %collective-permute-start.28) | collective-permute-done | bytes 1146912 | tf_op jit(solution)/shard_map/ppermute | solution.py:281
  790.7 1.8 fusion.9
  794.4 6.4 psum.7
  801.6 10.0 %fusion.17 = (bf16[2,640,896]{2,1,0:T(8,128)(2,1)}, f32[2,640,896]{2,1,0:T(8,128)}, f32[2,640,896]{2,1,0:T(8,128)}) fusion(bf16[2,640,896]{2,1,0:T(8,128)(2,1)} %refs_2_.5, f32[]{:T(128)S(6)} %min_shard_map.3, bf16[1,640,896]{2,1,0:T(8,128)(2,1)S(1)} %fusion.24, bf16[1,640,896]{2,1,0:T(8,128)(2,1)} %copy-done.4, f32[2,640,896]{2,1,0:T(8,128)} %param.21, ...), kind=kLoop, calls=%fused_computation.32 | loop fusion | flops 22937600 | bytes 25231364 | tf_op jit(solution)/shard_map/convert_element_type | solution.py:303
  811.6 8.8 %fusion.8 = (bf16[2,224,2560]{2,1,0:T(8,128)(2,1)}, f32[2,224,2560]{2,1,0:T(8,128)}, f32[2,224,2560]{2,1,0:T(8,128)}) fusion(bf16[2,224,2560]{2,1,0:T(8,128)(2,1)S(1)} %copy-done.7, f32[]{:T(128)S(6)} %min_shard_map.3, bf16[1,224,2560]{2,1,0:T(8,128)(2,1)S(1)} %copy-done.6, bf16[1,224,2560]{2,1,0:T(8,128)(2,1)S(1)} %maximum_bitcast_fusion, ...), kind=kLoop, calls=%fused_computation.23 | loop fusion | flops 22937600 | bytes 25231364 | tf_op jit(solution)/shard_map/convert_element_type | solution.py:303
  820.5 5.6 fusion.14
  (141 shorter events, 19.8 us)
Async XLA Ops:
  5.7 77.8 %collective-permute-start.1 = (bf16[224,2560]{1,0:T(8,128)(2,1)}, bf16[224,2560]{1,0:T(8,128)(2,1)}, u32[]{:S(2)}, u32[]{:S(2)}) collective-permute-start(bf16[224,2560]{1,0:T(8,128)(2,1)} %fusion.28), channel_id=1, source_target_pairs={{0,2},{1,3},{2,0},{3,1},{4,6},{5,7},{6,4},{7,5}} | collective-permute-start | bytes 3440648 | tf_op jit(solution)/shard_map/ppermute | solution.py:277
  14.1 33.3 %collective-permute-start.6 = (bf16[320,896]{1,0:T(8,128)(2,1)S(1)}, bf16[320,896]{1,0:T(8,128)(2,1)S(1)}, u32[]{:S(2)}, u32[]{:S(2)}) collective-permute-start(bf16[320,896]{1,0:T(8,128)(2,1)S(1)} %dynamic-slice_bitcast_fusion.1), channel_id=1, source_target_pairs={{0,2},{1,3},{2,0},{3,1},{4,6},{5,7},{6,4},{7,5}} | collective-permute-start | bytes 1720328 | tf_op jit(solution)/shard_map/ppermute | solution.py:277
  14.2 35.3 %copy-start.1 = (bf16[1,224,2560]{2,1,0:T(8,128)(2,1)S(1)}, bf16[1,224,2560]{2,1,0:T(8,128)(2,1)}, u32[]{:S(2)}) copy-start(bf16[1,224,2560]{2,1,0:T(8,128)(2,1)} %copy-done) | copy-start | bytes 3440644
  14.6 70.6 %collective-permute-start.11 = (bf16[224,2560]{1,0:T(8,128)(2,1)S(1)}, bf16[224,2560]{1,0:T(8,128)(2,1)}, u32[]{:S(2)}, u32[]{:S(2)}) collective-permute-start(bf16[224,2560]{1,0:T(8,128)(2,1)S(1)} %fusion.26), channel_id=1, source_target_pairs={{0,2},{1,3},{2,0},{3,1},{4,6},{5,7},{6,4},{7,5}} | collective-permute-start | bytes 3440648 | tf_op jit(solution)/shard_map/ppermute | solution.py:277
  16.7 68.6 %copy-start.14 = (bf16[640,896]{1,0:T(8,128)(2,1)S(1)}, bf16[640,896]{1,0:T(8,128)(2,1)}, u32[]{:S(2)}) copy-start(bf16[640,896]{1,0:T(8,128)(2,1)} %get-tuple-element.69) | copy-start | bytes 3440644
  16.7 66.8 %collective-permute-start.16 = (bf16[320,896]{1,0:T(8,128)(2,1)S(1)}, bf16[320,896]{1,0:T(8,128)(2,1)S(1)}, u32[]{:S(2)}, u32[]{:S(2)}) collective-permute-start(bf16[320,896]{1,0:T(8,128)(2,1)S(1)} %dynamic-slice_bitcast_fusion), channel_id=1, source_target_pairs={{0,2},{1,3},{2,0},{3,1},{4,6},{5,7},{6,4},{7,5}} | collective-permute-start | bytes 1720328 | tf_op jit(solution)/shard_map/ppermute | solution.py:277
  47.4 38.0 %collective-permute-start.8 = (bf16[320,896]{1,0:T(8,128)(2,1)S(1)}, bf16[320,896]{1,0:T(8,128)(2,1)S(1)}, u32[]{:S(2)}, u32[]{:S(2)}) collective-permute-start(bf16[320,896]{1,0:T(8,128)(2,1)S(1)} %collective-permute-done.6.refs_9_), channel_id=1, source_target_pairs={{0,1},{1,0},{2,3},{3,2},{4,5},{5,4},{6,7},{7,6}} | collective-permute-start | bytes 1720328 | tf_op jit(solution)/shard_map/ppermute | solution.py:273
  47.4 38.3 %collective-permute-start.7 = (bf16[320,896]{1,0:T(8,128)(2,1)S(1)}, bf16[320,896]{1,0:T(8,128)(2,1)}, u32[]{:S(2)}, u32[]{:S(2)}) collective-permute-start(bf16[320,896]{1,0:T(8,128)(2,1)S(1)} %collective-permute-done.6.refs_9_), channel_id=1, source_target_pairs={{0,4},{4,0},{1,5},{5,1},{2,6},{6,2},{3,7},{7,3}} | collective-permute-start | bytes 1720328 | tf_op jit(solution)/shard_map/ppermute | solution.py:281
  83.4 41.8 %copy-start.24 = (bf16[320,896]{1,0:T(8,128)(2,1)}, bf16[320,896]{1,0:T(8,128)(2,1)S(1)}, u32[]{:S(2)}) copy-start(bf16[320,896]{1,0:T(8,128)(2,1)S(1)} %collective-permute-done.16.refs_9_) | copy-start | bytes 1720324
  83.4 66.9 %collective-permute-start = (bf16[2,224,2560]{2,1,0:T(8,128)(2,1)}, bf16[2,224,2560]{2,1,0:T(8,128)(2,1)}, u32[]{:S(2)}, u32[]{:S(2)}) collective-permute-start(bf16[2,224,2560]{2,1,0:T(8,128)(2,1)} %pad_maximum_fusion), channel_id=1, source_target_pairs={{0,1},{1,0},{2,3},{3,2},{4,5},{5,4},{6,7},{7,6}} | collective-permute-start | bytes 6881288 | tf_op jit(solution)/shard_map/ppermute | solution.py:273
  83.4 41.7 %collective-permute-start.2 = (bf16[224,2560]{1,0:T(8,128)(2,1)}, bf16[224,2560]{1,0:T(8,128)(2,1)S(1)}, u32[]{:S(2)}, u32[]{:S(2)}) collective-permute-start(bf16[224,2560]{1,0:T(8,128)(2,1)} %collective-permute-done.1.refs_4_), channel_id=1, source_target_pairs={{0,4},{4,0},{1,5},{5,1},{2,6},{6,2},{3,7},{7,3}} | collective-permute-start | bytes 3440648 | tf_op jit(solution)/shard_map/ppermute | solution.py:281
  85.2 40.0 %collective-permute-start.5 = (bf16[640,896]{1,0:T(8,128)(2,1)S(1)}, bf16[640,896]{1,0:T(8,128)(2,1)S(1)}, u32[]{:S(2)}, u32[]{:S(2)}) collective-permute-start(bf16[640,896]{1,0:T(8,128)(2,1)S(1)} %copy-done.14), channel_id=1, source_target_pairs={{0,1},{1,0},{2,3},{3,2},{4,5},{5,4},{6,7},{7,6}} | collective-permute-start | bytes 3440648 | tf_op jit(solution)/shard_map/ppermute | solution.py:273
  85.4 39.8 %copy-start.23 = (bf16[320,896]{1,0:T(8,128)(2,1)}, bf16[320,896]{1,0:T(8,128)(2,1)S(1)}, u32[]{:S(2)}) copy-start(bf16[320,896]{1,0:T(8,128)(2,1)S(1)} %collective-permute-done.8.refs_11_) | copy-start | bytes 1720324
  85.4 4.9 collective-permute-start.18
  85.8 37.7 %collective-permute-start.17 = (bf16[320,896]{1,0:T(8,128)(2,1)S(1)}, bf16[320,896]{1,0:T(8,128)(2,1)}, u32[]{:S(2)}, u32[]{:S(2)}) collective-permute-start(bf16[320,896]{1,0:T(8,128)(2,1)S(1)} %collective-permute-done.16.refs_9_), channel_id=1, source_target_pairs={{0,4},{4,0},{1,5},{5,1},{2,6},{6,2},{3,7},{7,3}} | collective-permute-start | bytes 1720328 | tf_op jit(solution)/shard_map/ppermute | solution.py:281
  90.3 34.9 %copy-start.25 = (bf16[320,896]{1,0:T(8,128)(2,1)}, bf16[320,896]{1,0:T(8,128)(2,1)S(1)}, u32[]{:S(2)}) copy-start(bf16[320,896]{1,0:T(8,128)(2,1)S(1)} %collective-permute-done.18.refs_11_) | copy-start | bytes 1720324
  90.3 38.7 %collective-permute-start.3 = (bf16[224,2560]{1,0:T(8,128)(2,1)}, bf16[224,2560]{1,0:T(8,128)(2,1)}, u32[]{:S(2)}, u32[]{:S(2)}) collective-permute-start(bf16[224,2560]{1,0:T(8,128)(2,1)} %collective-permute-done.1.refs_4_), channel_id=1, source_target_pairs={{0,1},{1,0},{2,3},{3,2},{4,5},{5,4},{6,7},{7,6}} | collective-permute-start | bytes 3440648 | tf_op jit(solution)/shard_map/ppermute | solution.py:273
  123.4 26.9 %collective-permute-start.12 = (bf16[224,2560]{1,0:T(8,128)(2,1)}, bf16[224,2560]{1,0:T(8,128)(2,1)}, u32[]{:S(2)}, u32[]{:S(2)}) collective-permute-start(bf16[224,2560]{1,0:T(8,128)(2,1)} %collective-permute-done.11.refs_4_), channel_id=1, source_target_pairs={{0,4},{4,0},{1,5},{5,1},{2,6},{6,2},{3,7},{7,3}} | collective-permute-start | bytes 3440648 | tf_op jit(solution)/shard_map/ppermute | solution.py:281
  125.2 25.7 %collective-permute-start.4 = (bf16[224,2560]{1,0:T(8,128)(2,1)S(1)}, bf16[224,2560]{1,0:T(8,128)(2,1)}, u32[]{:S(2)}, u32[]{:S(2)}) collective-permute-start(bf16[224,2560]{1,0:T(8,128)(2,1)S(1)} %collective-permute-done.2.refs_5_), channel_id=1, source_target_pairs={{0,1},{1,0},{2,3},{3,2},{4,5},{5,4},{6,7},{7,6}} | collective-permute-start | bytes 3440648 | tf_op jit(solution)/shard_map/ppermute | solution.py:273
  126.3 2.7 collective-permute-start.9
  129.0 102.7 %collective-permute-start.10 = (bf16[2,224,2560]{2,1,0:T(8,128)(2,1)}, bf16[2,224,2560]{2,1,0:T(8,128)(2,1)}, u32[]{:S(2)}, u32[]{:S(2)}) collective-permute-start(bf16[2,224,2560]{2,1,0:T(8,128)(2,1)} %pad_maximum_fusion.1), channel_id=1, source_target_pairs={{0,1},{1,0},{2,3},{3,2},{4,5},{5,4},{6,7},{7,6}} | collective-permute-start | bytes 6881288 | tf_op jit(solution)/shard_map/ppermute | solution.py:273
  129.0 102.5 %collective-permute-start.15 = (bf16[640,896]{1,0:T(8,128)(2,1)}, bf16[640,896]{1,0:T(8,128)(2,1)}, u32[]{:S(2)}, u32[]{:S(2)}) collective-permute-start(bf16[640,896]{1,0:T(8,128)(2,1)} %get-tuple-element.70), channel_id=1, source_target_pairs={{0,1},{1,0},{2,3},{3,2},{4,5},{5,4},{6,7},{7,6}} | collective-permute-start | bytes 3440648 | tf_op jit(solution)/shard_map/ppermute | solution.py:273
  150.4 81.2 %collective-permute-start.13 = (bf16[224,2560]{1,0:T(8,128)(2,1)}, bf16[224,2560]{1,0:T(8,128)(2,1)}, u32[]{:S(2)}, u32[]{:S(2)}) collective-permute-start(bf16[224,2560]{1,0:T(8,128)(2,1)} %collective-permute-done.11.refs_4_), channel_id=1, source_target_pairs={{0,1},{1,0},{2,3},{3,2},{4,5},{5,4},{6,7},{7,6}} | collective-permute-start | bytes 3440648 | tf_op jit(solution)/shard_map/ppermute | solution.py:273
  150.4 81.2 %collective-permute-start.19 = (bf16[320,896]{1,0:T(8,128)(2,1)}, bf16[320,896]{1,0:T(8,128)(2,1)}, u32[]{:S(2)}, u32[]{:S(2)}) collective-permute-start(bf16[320,896]{1,0:T(8,128)(2,1)} %collective-permute-done.17.refs_10_), channel_id=1, source_target_pairs={{0,1},{1,0},{2,3},{3,2},{4,5},{5,4},{6,7},{7,6}} | collective-permute-start | bytes 1720328 | tf_op jit(solution)/shard_map/ppermute | solution.py:273
  150.9 80.7 %collective-permute-start.14 = (bf16[224,2560]{1,0:T(8,128)(2,1)}, bf16[224,2560]{1,0:T(8,128)(2,1)}, u32[]{:S(2)}, u32[]{:S(2)}) collective-permute-start(bf16[224,2560]{1,0:T(8,128)(2,1)} %collective-permute-done.12.refs_5_), channel_id=1, source_target_pairs={{0,1},{1,0},{2,3},{3,2},{4,5},{5,4},{6,7},{7,6}} | collective-permute-start | bytes 3440648 | tf_op jit(solution)/shard_map/ppermute | solution.py:273
  551.8 31.2 %collective-permute-start.23 = (bf16[448,1280]{1,0:T(8,128)(2,1)}, bf16[448,1280]{1,0:T(8,128)(2,1)}, u32[]{:S(2)}, u32[]{:S(2)}) collective-permute-start(bf16[448,1280]{1,0:T(8,128)(2,1)} %get-tuple-element.44), channel_id=1, source_target_pairs={{0,1},{1,0},{2,3},{3,2},{4,5},{5,4},{6,7},{7,6}} | collective-permute-start | bytes 3440648 | tf_op jit(solution)/shard_map/ppermute | solution.py:273
  552.3 32.3 %collective-permute-start.20 = (bf16[448,1280]{1,0:T(8,128)(2,1)}, bf16[448,1280]{1,0:T(8,128)(2,1)}, u32[]{:S(2)}, u32[]{:S(2)}) collective-permute-start(bf16[448,1280]{1,0:T(8,128)(2,1)} %get-tuple-element.42), channel_id=1, source_target_pairs={{0,1},{1,0},{2,3},{3,2},{4,5},{5,4},{6,7},{7,6}} | collective-permute-start | bytes 3440648 | tf_op jit(solution)/shard_map/ppermute | solution.py:273
  567.2 19.3 %collective-permute-start.32 = (bf16[448,1280]{1,0:T(8,128)(2,1)}, bf16[448,1280]{1,0:T(8,128)(2,1)}, u32[]{:S(2)}, u32[]{:S(2)}) collective-permute-start(bf16[448,1280]{1,0:T(8,128)(2,1)} %get-tuple-element.52), channel_id=1, source_target_pairs={{0,1},{1,0},{2,3},{3,2},{4,5},{5,4},{6,7},{7,6}} | collective-permute-start | bytes 3440648 | tf_op jit(solution)/shard_map/ppermute | solution.py:273
  582.5 5.7 copy-start.17
  582.5 6.9 collective-permute-start.29
  582.6 60.4 %collective-permute-start.41 = (bf16[1280,896]{1,0:T(8,128)(2,1)}, bf16[1280,896]{1,0:T(8,128)(2,1)S(1)}, u32[]{:S(2)}, u32[]{:S(2)}) collective-permute-start(bf16[1280,896]{1,0:T(8,128)(2,1)} %by_down.7), channel_id=1, source_target_pairs={{0,1},{1,0},{2,3},{3,2},{4,5},{5,4},{6,7},{7,6}} | collective-permute-start | bytes 6881288 | tf_op jit(solution)/shard_map/ppermute | solution.py:273
  583.0 57.3 %collective-permute-start.35 = (bf16[448,2560]{1,0:T(8,128)(2,1)}, bf16[448,2560]{1,0:T(8,128)(2,1)S(1)}, u32[]{:S(2)}, u32[]{:S(2)}) collective-permute-start(bf16[448,2560]{1,0:T(8,128)(2,1)} %get-tuple-element.54), channel_id=1, source_target_pairs={{0,1},{1,0},{2,3},{3,2},{4,5},{5,4},{6,7},{7,6}} | collective-permute-start | bytes 6881288 | tf_op jit(solution)/shard_map/ppermute | solution.py:273
  583.1 6.7 copy-start.15
  584.6 56.4 %collective-permute-start.26 = (bf16[448,2560]{1,0:T(8,128)(2,1)}, bf16[448,2560]{1,0:T(8,128)(2,1)S(1)}, u32[]{:S(2)}, u32[]{:S(2)}) collective-permute-start(bf16[448,2560]{1,0:T(8,128)(2,1)} %get-tuple-element.47), channel_id=1, source_target_pairs={{0,1},{1,0},{2,3},{3,2},{4,5},{5,4},{6,7},{7,6}} | collective-permute-start | bytes 6881288 | tf_op jit(solution)/shard_map/ppermute | solution.py:273
  585.0 19.0 %copy-start.18 = (bf16[448,1280]{1,0:T(8,128)(2,1)S(1)}, bf16[448,1280]{1,0:T(8,128)(2,1)}, u32[]{:S(2)}) copy-start(bf16[448,1280]{1,0:T(8,128)(2,1)} %get-tuple-element.43) | copy-start | bytes 3440644
  586.5 15.9 %collective-permute-start.24 = (bf16[224,1280]{1,0:T(8,128)(2,1)S(1)}, bf16[224,1280]{1,0:T(8,128)(2,1)S(1)}, u32[]{:S(2)}, u32[]{:S(2)}) collective-permute-start(bf16[224,1280]{1,0:T(8,128)(2,1)S(1)} %add_convert_fusion.20), channel_id=1, source_target_pairs={{0,2},{1,3},{2,0},{3,1},{4,6},{5,7},{6,4},{7,5}} | collective-permute-start | bytes 1720328 | tf_op jit(solution)/shard_map/ppermute | solution.py:277
  589.4 26.9 %copy-start.16 = (bf16[448,1280]{1,0:T(8,128)(2,1)S(1)}, bf16[448,1280]{1,0:T(8,128)(2,1)}, u32[]{:S(2)}) copy-start(bf16[448,1280]{1,0:T(8,128)(2,1)} %get-tuple-element.41) | copy-start | bytes 3440644
  589.4 25.2 %collective-permute-start.21 = (bf16[224,1280]{1,0:T(8,128)(2,1)S(1)}, bf16[224,1280]{1,0:T(8,128)(2,1)S(1)}, u32[]{:S(2)}, u32[]{:S(2)}) collective-permute-start(bf16[224,1280]{1,0:T(8,128)(2,1)S(1)} %add_convert_fusion.23), channel_id=1, source_target_pairs={{0,2},{1,3},{2,0},{3,1},{4,6},{5,7},{6,4},{7,5}} | collective-permute-start | bytes 1720328 | tf_op jit(solution)/shard_map/ppermute | solution.py:277
  590.0 37.0 %copy-start.19 = (bf16[1280,896]{1,0:T(8,128)(2,1)S(1)}, bf16[1280,896]{1,0:T(8,128)(2,1)}, u32[]{:S(2)}) copy-start(bf16[1280,896]{1,0:T(8,128)(2,1)} %by_down.5) | copy-start | bytes 6881284
  602.4 24.6 %collective-permute-start.33 = (bf16[224,1280]{1,0:T(8,128)(2,1)S(1)}, bf16[224,1280]{1,0:T(8,128)(2,1)S(1)}, u32[]{:S(2)}, u32[]{:S(2)}) collective-permute-start(bf16[224,1280]{1,0:T(8,128)(2,1)S(1)} %add_convert_fusion.14), channel_id=1, source_target_pairs={{0,2},{1,3},{2,0},{3,1},{4,6},{5,7},{6,4},{7,5}} | collective-permute-start | bytes 1720328 | tf_op jit(solution)/shard_map/ppermute | solution.py:277
  614.7 23.7 %collective-permute-start.30 = (bf16[224,1280]{1,0:T(8,128)(2,1)S(1)}, bf16[224,1280]{1,0:T(8,128)(2,1)S(1)}, u32[]{:S(2)}, u32[]{:S(2)}) collective-permute-start(bf16[224,1280]{1,0:T(8,128)(2,1)S(1)} %add_convert_fusion.17), channel_id=1, source_target_pairs={{0,2},{1,3},{2,0},{3,1},{4,6},{5,7},{6,4},{7,5}} | collective-permute-start | bytes 1720328 | tf_op jit(solution)/shard_map/ppermute | solution.py:277
  617.7 23.0 %copy-start.11 = (bf16[448,2560]{1,0:T(8,128)(2,1)S(1)}, bf16[448,2560]{1,0:T(8,128)(2,1)}, u32[]{:S(2)}) copy-start(bf16[448,2560]{1,0:T(8,128)(2,1)} %get-tuple-element.53) | copy-start | bytes 6881284
  627.0 16.7 %collective-permute-start.38 = (bf16[1280,896]{1,0:T(8,128)(2,1)S(1)}, bf16[1280,896]{1,0:T(8,128)(2,1)S(1)}, u32[]{:S(2)}, u32[]{:S(2)}) collective-permute-start(bf16[1280,896]{1,0:T(8,128)(2,1)S(1)} %copy-done.19), channel_id=1, source_target_pairs={{0,1},{1,0},{2,3},{3,2},{4,5},{5,4},{6,7},{7,6}} | collective-permute-start | bytes 6881288 | tf_op jit(solution)/shard_map/ppermute | solution.py:273
  638.4 15.9 %collective-permute-start.25 = (bf16[224,1280]{1,0:T(8,128)(2,1)S(1)}, bf16[224,1280]{1,0:T(8,128)(2,1)S(1)}, u32[]{:S(2)}, u32[]{:S(2)}) collective-permute-start(bf16[224,1280]{1,0:T(8,128)(2,1)S(1)} %add_convert_fusion.19), channel_id=1, source_target_pairs={{0,4},{4,0},{1,5},{5,1},{2,6},{6,2},{3,7},{7,3}} | collective-permute-start | bytes 1720328 | tf_op jit(solution)/shard_map/ppermute | solution.py:281
  640.4 26.2 %collective-permute-start.22 = (bf16[224,1280]{1,0:T(8,128)(2,1)S(1)}, bf16[224,1280]{1,0:T(8,128)(2,1)S(1)}, u32[]{:S(2)}, u32[]{:S(2)}) collective-permute-start(bf16[224,1280]{1,0:T(8,128)(2,1)S(1)} %add_convert_fusion.22), channel_id=1, source_target_pairs={{0,4},{4,0},{1,5},{5,1},{2,6},{6,2},{3,7},{7,3}} | collective-permute-start | bytes 1720328 | tf_op jit(solution)/shard_map/ppermute | solution.py:281
  641.0 37.8 %collective-permute-start.34 = (bf16[224,1280]{1,0:T(8,128)(2,1)S(1)}, bf16[224,1280]{1,0:T(8,128)(2,1)S(1)}, u32[]{:S(2)}, u32[]{:S(2)}) collective-permute-start(bf16[224,1280]{1,0:T(8,128)(2,1)S(1)} %add_convert_fusion.13), channel_id=1, source_target_pairs={{0,4},{4,0},{1,5},{5,1},{2,6},{6,2},{3,7},{7,3}} | collective-permute-start | bytes 1720328 | tf_op jit(solution)/shard_map/ppermute | solution.py:281
  643.0 46.3 %collective-permute-start.31 = (bf16[224,1280]{1,0:T(8,128)(2,1)S(1)}, bf16[224,1280]{1,0:T(8,128)(2,1)S(1)}, u32[]{:S(2)}, u32[]{:S(2)}) collective-permute-start(bf16[224,1280]{1,0:T(8,128)(2,1)S(1)} %add_convert_fusion.16), channel_id=1, source_target_pairs={{0,4},{4,0},{1,5},{5,1},{2,6},{6,2},{3,7},{7,3}} | collective-permute-start | bytes 1720328 | tf_op jit(solution)/shard_map/ppermute | solution.py:281
  643.7 46.0 %collective-permute-start.42 = (bf16[640,896]{1,0:T(8,128)(2,1)S(1)}, bf16[640,896]{1,0:T(8,128)(2,1)S(1)}, u32[]{:S(2)}, u32[]{:S(2)}) collective-permute-start(bf16[640,896]{1,0:T(8,128)(2,1)S(1)} %add_convert_fusion.2), channel_id=1, source_target_pairs={{0,2},{1,3},{2,0},{3,1},{4,6},{5,7},{6,4},{7,5}} | collective-permute-start | bytes 3440648 | tf_op jit(solution)/shard_map/ppermute | solution.py:277
  654.2 42.2 %collective-permute-start.39 = (bf16[640,896]{1,0:T(8,128)(2,1)S(1)}, bf16[640,896]{1,0:T(8,128)(2,1)S(1)}, u32[]{:S(2)}, u32[]{:S(2)}) collective-permute-start(bf16[640,896]{1,0:T(8,128)(2,1)S(1)} %add_convert_fusion.5), channel_id=1, source_target_pairs={{0,2},{1,3},{2,0},{3,1},{4,6},{5,7},{6,4},{7,5}} | collective-permute-start | bytes 3440648 | tf_op jit(solution)/shard_map/ppermute | solution.py:277
  666.5 54.5 %collective-permute-start.36 = (bf16[224,2560]{1,0:T(8,128)(2,1)S(1)}, bf16[224,2560]{1,0:T(8,128)(2,1)S(1)}, u32[]{:S(2)}, u32[]{:S(2)}) collective-permute-start(bf16[224,2560]{1,0:T(8,128)(2,1)S(1)} %add_convert_fusion.8), channel_id=1, source_target_pairs={{0,2},{1,3},{2,0},{3,1},{4,6},{5,7},{6,4},{7,5}} | collective-permute-start | bytes 3440648 | tf_op jit(solution)/shard_map/ppermute | solution.py:277
  678.8 64.1 %collective-permute-start.27 = (bf16[224,2560]{1,0:T(8,128)(2,1)S(1)}, bf16[224,2560]{1,0:T(8,128)(2,1)S(1)}, u32[]{:S(2)}, u32[]{:S(2)}) collective-permute-start(bf16[224,2560]{1,0:T(8,128)(2,1)S(1)} %add_convert_fusion.11), channel_id=1, source_target_pairs={{0,2},{1,3},{2,0},{3,1},{4,6},{5,7},{6,4},{7,5}} | collective-permute-start | bytes 3440648 | tf_op jit(solution)/shard_map/ppermute | solution.py:277
  690.1 54.7 %collective-permute-start.43 = (bf16[640,896]{1,0:T(8,128)(2,1)S(1)}, bf16[640,896]{1,0:T(8,128)(2,1)S(1)}, u32[]{:S(2)}, u32[]{:S(2)}) collective-permute-start(bf16[640,896]{1,0:T(8,128)(2,1)S(1)} %add_convert_fusion.1), channel_id=1, source_target_pairs={{0,4},{4,0},{1,5},{5,1},{2,6},{6,2},{3,7},{7,3}} | collective-permute-start | bytes 3440648 | tf_op jit(solution)/shard_map/ppermute | solution.py:281
  696.8 48.3 %collective-permute-start.40 = (bf16[640,896]{1,0:T(8,128)(2,1)S(1)}, bf16[640,896]{1,0:T(8,128)(2,1)S(1)}, u32[]{:S(2)}, u32[]{:S(2)}) collective-permute-start(bf16[640,896]{1,0:T(8,128)(2,1)S(1)} %add_convert_fusion.4), channel_id=1, source_target_pairs={{0,4},{4,0},{1,5},{5,1},{2,6},{6,2},{3,7},{7,3}} | collective-permute-start | bytes 3440648 | tf_op jit(solution)/shard_map/ppermute | solution.py:281
  721.4 46.0 %collective-permute-start.37 = (bf16[224,2560]{1,0:T(8,128)(2,1)S(1)}, bf16[224,2560]{1,0:T(8,128)(2,1)S(1)}, u32[]{:S(2)}, u32[]{:S(2)}) collective-permute-start(bf16[224,2560]{1,0:T(8,128)(2,1)S(1)} %add_convert_fusion.7), channel_id=1, source_target_pairs={{0,4},{4,0},{1,5},{5,1},{2,6},{6,2},{3,7},{7,3}} | collective-permute-start | bytes 3440648 | tf_op jit(solution)/shard_map/ppermute | solution.py:281
  743.4 46.1 %collective-permute-start.28 = (bf16[224,2560]{1,0:T(8,128)(2,1)S(1)}, bf16[224,2560]{1,0:T(8,128)(2,1)S(1)}, u32[]{:S(2)}, u32[]{:S(2)}) collective-permute-start(bf16[224,2560]{1,0:T(8,128)(2,1)S(1)} %add_convert_fusion.10), channel_id=1, source_target_pairs={{0,4},{4,0},{1,5},{5,1},{2,6},{6,2},{3,7},{7,3}} | collective-permute-start | bytes 3440648 | tf_op jit(solution)/shard_map/ppermute | solution.py:281
  767.7 22.0 %copy-start.2 = (bf16[1,224,2560]{2,1,0:T(8,128)(2,1)}, bf16[1,224,2560]{2,1,0:T(8,128)(2,1)S(1)}, u32[]{:S(2)}) copy-start(bf16[1,224,2560]{2,1,0:T(8,128)(2,1)S(1)} %fusion.22) | copy-start | bytes 3440644
  801.6 10.0 %copy-start.6 = (bf16[1,224,2560]{2,1,0:T(8,128)(2,1)S(1)}, bf16[1,224,2560]{2,1,0:T(8,128)(2,1)}, u32[]{:S(2)}) copy-start(bf16[1,224,2560]{2,1,0:T(8,128)(2,1)} %copy-done.5) | copy-start | bytes 3440644
  801.6 10.0 %copy-start.7 = (bf16[2,224,2560]{2,1,0:T(8,128)(2,1)S(1)}, bf16[2,224,2560]{2,1,0:T(8,128)(2,1)}, u32[]{:S(2)}) copy-start(bf16[2,224,2560]{2,1,0:T(8,128)(2,1)} %refs_0_.5) | copy-start | bytes 6881284
  801.6 18.8 %slice-start = ((s8[4587520]{0:T(1024)(128)(4,1)}), s8[4194304]{0:T(1024)(128)(4,1)S(1)}, s32[]{:S(2)}) async-start(s8[4587520]{0:T(1024)(128)(4,1)} %bitcast.28), calls=%async_computation | async-start | bytes 8388608
  801.6 18.8 %slice-start.2 = ((s8[4587520]{0:T(1024)(128)(4,1)}), s8[4194304]{0:T(1024)(128)(4,1)S(1)}, s32[]{:S(2)}) async-start(s8[4587520]{0:T(1024)(128)(4,1)} %bitcast.30), calls=%async_computation.2 | async-start | bytes 8388608
  811.6 8.8 %copy-start.3 = (bf16[1,224,2560]{2,1,0:T(8,128)(2,1)S(1)}, bf16[1,224,2560]{2,1,0:T(8,128)(2,1)}, u32[]{:S(2)}) copy-start(bf16[1,224,2560]{2,1,0:T(8,128)(2,1)} %copy-done.2) | copy-start | bytes 3440644
  811.6 8.8 %copy-start.8 = (bf16[2,224,2560]{2,1,0:T(8,128)(2,1)S(1)}, bf16[2,224,2560]{2,1,0:T(8,128)(2,1)}, u32[]{:S(2)}) copy-start(bf16[2,224,2560]{2,1,0:T(8,128)(2,1)} %refs_1_.5) | copy-start | bytes 6881284
  811.6 8.8 %slice-start.1 = ((s8[4587520]{0:T(1024)(128)(4,1)}), s8[393216]{0:T(1024)(128)(4,1)S(1)}, s32[]{:S(2)}) async-start(s8[4587520]{0:T(1024)(128)(4,1)} %bitcast.28), calls=%async_computation.1 | async-start | bytes 786432
  811.6 8.8 %slice-start.3 = ((s8[4587520]{0:T(1024)(128)(4,1)}), s8[393216]{0:T(1024)(128)(4,1)S(1)}, s32[]{:S(2)}) async-start(s8[4587520]{0:T(1024)(128)(4,1)} %bitcast.30), calls=%async_computation.3 | async-start | bytes 786432
  (10 other events, 23.1 us)
